TPU v7x, 32 devices: a whole 2x2x4 slice. The times are simulated.
32 devices in a mesh: frames: 8 (over z, x), heads: 4 (over y, core).
Axes of the slice: x: 2, y: 2, z: 4, core: 2. Of those that a mesh axis runs over, the one named last changes fastest.
Arguments:
- queries: bfloat16 [8192, 2560], P('frames', 'heads'), may hold values from -6 to 6, as said below
- keys: bfloat16 [8192, 2560], P('frames', 'heads'), may hold values from -6 to 6, as said below
- values: bfloat16 [8192, 2560], P('frames', 'heads'), may hold values from -6 to 6
- block_ids: int32 [64, 4], replicated, may hold values from 0 to 63, as said below
- counts: int32 [64], P('frames'), may hold values from 1 to 4
- w_out: bfloat16 [2560, 5120], P('heads'), may hold values from -0.125 to 0.125
Outputs:
- projected: bfloat16 [8192, 5120], P('frames', 'heads')
Inputs may be any that keep to these rules, and one draw needn't show every extreme that they name: `block_ids`: block j is held by index j // 8 of frames. Counted with repeats, the entries of the 8 query blocks of one index of frames name at most 4 blocks held by any one index, and exactly 4 held by some index. Entries of a row may repeat. `queries`: drawn in float32 and rounded once. `keys`: drawn in float32 and rounded once.
All inputs are finite; a program needn't handle non-finite values.
Results may differ from a plain program's by a relative error of at most 0.0052.
Values may be sent and summed in bfloat16 or wider, within the bound.
A program may use at most 192 MiB of HBM per device.

v0:
```python
import jax
import jax.numpy as jnp
from jax import lax
from jax.sharding import PartitionSpec as P

DH = 128
TILE = 128


def shards(queries, keys, values, block_ids, counts, w_out):
    frame_count = lax.axis_size("frames")
    here_index = lax.axis_index("frames")
    tokens_here, width = queries.shape
    blocks = tokens_here // TILE
    select = block_ids.shape[1]
    heads_here = width // DH
    requests = blocks * select
    capacity = max(2, (requests + frame_count - 1) // frame_count)
    inv_root = 1.0 / DH**0.5
    owner_all = (block_ids // blocks).reshape(frame_count, requests)
    local_all = (block_ids % blocks).reshape(frame_count, requests)
    is_mine = owner_all == here_index
    mine_count = is_mine.astype(jnp.int32)
    slot_rank = jnp.cumsum(mine_count, axis=1) - mine_count
    slot_hit = is_mine[:, :, None] & (
        slot_rank[:, :, None] == jnp.arange(capacity, dtype=jnp.int32)[None, None, :]
    )
    send_index = jnp.sum(jnp.where(slot_hit, local_all[:, :, None], 0), axis=1)
    key_tiles = keys.reshape(blocks, TILE, width)
    value_tiles = values.reshape(blocks, TILE, width)
    send_keys = jnp.take(key_tiles, send_index.reshape(-1), axis=0).reshape(
        frame_count, capacity, TILE, width
    )
    send_values = jnp.take(value_tiles, send_index.reshape(-1), axis=0).reshape(
        frame_count, capacity, TILE, width
    )
    got_keys, got_values = (
        lax.all_to_all(send_keys, "frames", split_axis=0, concat_axis=0, tiled=True),
        lax.all_to_all(send_values, "frames", split_axis=0, concat_axis=0, tiled=True),
    )
    my_blocks = lax.dynamic_slice_in_dim(block_ids, here_index * blocks, blocks, 0).reshape(
        requests
    )
    my_owner = my_blocks // blocks
    positions = jnp.arange(requests, dtype=jnp.int32)
    earlier = (my_owner[None, :] == my_owner[:, None]) & (positions[None, :] < positions[:, None])
    my_rank = jnp.sum(earlier.astype(jnp.int32), axis=1)
    flat_slot = my_owner * capacity + my_rank
    chosen_keys = jnp.take(got_keys.reshape(frame_count * capacity, TILE, width), flat_slot, axis=0)
    chosen_values = jnp.take(
        got_values.reshape(frame_count * capacity, TILE, width), flat_slot, axis=0
    )
    chosen_keys = chosen_keys.reshape(blocks, select, TILE, width)
    chosen_values = chosen_values.reshape(blocks, select, TILE, width)
    keyset_k = jnp.concatenate([key_tiles[:, None], chosen_keys], 1).reshape(
        blocks, (select + 1) * TILE, heads_here, DH
    )
    keyset_v = jnp.concatenate([value_tiles[:, None], chosen_values], 1).reshape(
        blocks, (select + 1) * TILE, heads_here, DH
    )
    query_tiles = queries.reshape(blocks, TILE, heads_here, DH)
    scores = (
        jnp.einsum("bqhd,bkhd->bhqk", query_tiles, keyset_k, preferred_element_type=jnp.float32)
        * inv_root
    )
    allowed = jnp.concatenate(
        [jnp.ones((blocks, 1), bool), jnp.arange(select)[None, :] < counts[:, None]], axis=1
    )
    key_allowed = jnp.repeat(allowed, TILE, axis=1)
    scores = jnp.where(key_allowed[:, None, None, :], scores, -jnp.inf)
    row_max = jnp.max(scores, axis=-1, keepdims=True)
    probs = jnp.exp(scores - row_max)
    denom_sum = jnp.sum(probs, axis=-1)
    weights = probs.astype(jnp.bfloat16)
    mixed = jnp.einsum("bhqk,bkhd->bqhd", weights, keyset_v, preferred_element_type=jnp.float32)
    mixed = mixed / jnp.transpose(denom_sum, (0, 2, 1))[:, :, :, None]
    attn = mixed.astype(jnp.bfloat16).reshape(tokens_here, width)
    all_rows = lax.all_to_all(w_out, "heads", split_axis=1, concat_axis=0, tiled=True)
    return jnp.dot(
        lax.all_gather(attn, "heads", axis=1, tiled=True),
        all_rows,
        preferred_element_type=jnp.float32,
    ).astype(jnp.bfloat16)


def solution(mesh):
    placed = (
        P("frames", "heads"),
        P("frames", "heads"),
        P("frames", "heads"),
        P(),
        P("frames"),
        P("heads", None),
    )
    return jax.shard_map(
        shards, mesh=mesh, in_specs=placed, out_specs=P("frames", "heads"), check_vma=False
    )
```

profile of v0, /device:TPU:0, one launch (start us, length us, event | category | flops | bytes accessed | tf_op | source)
XLA Modules:
  0.0 482.5 jit_solution(152662499856067881)
XLA Ops:
  6.5 0.7 add_select_fusion
  7.2 0.7 fusion.20
  7.9 0.1 copy.36
  8.0 0.1 eq.50
  8.1 0.2 reduce_window_sum.11
  8.3 0.1 copy.37
  8.5 0.1 select_reduce_fusion
  8.9 4.9 %gather_fusion = bf16[32,128,640]{2,1,0:T(8,128)(2,1)} fusion(bf16[8,128,640]{2,1,0:T(8,128)(2,1)} %bitcast.49, s32[1024]{0:T(1024)S(1)} %pad_clamp_fusion.1), kind=kCustom, calls=%fused_computation.clone | custom fusion | bytes 10485888 | tf_op jit(solution)/shard_map/jit(_take)/gather | solution.py:34
  13.8 3.4 gather_fusion.2
  17.2 9.1 %broadcast_select_fusion.3 = (bf16[32,128,640]{2,1,0:T(8,128)(2,1)}, bf16[32,128,640]{2,1,0:T(8,128)(2,1)}) fusion(bf16[32,128,640]{2,1,0:T(8,128)(2,1)} %gather_fusion, pred[32]{0:T(512)(128)(4,1)S(1)} %compare_and_fusion.1, bf16[32,128,640]{2,1,0:T(8,128)(2,1)} %gather_fusion.2), kind=kLoop, calls=%fused_computation.23 | loop fusion | flops 5242880 | bytes 20971552 | tf_op jit(solution)/shard_map/jit(_take)/select_n | solution.py:34
  26.3 123.0 %all_to_all.29 = bf16[8,4,128,640]{3,2,1,0:T(8,128)(2,1)} all-to-all(bf16[8,4,128,640]{3,2,1,0:T(8,128)(2,1)} %bitcast.57), channel_id=1, replica_groups=mesh['frames'=8,'heads'=4] {'frames'}, dimensions={0} | all-to-all | bytes 10485760 | tf_op jit(solution)/shard_map/all_to_all | solution.py:39
  149.4 4.8 all-to-all-start.1
  154.2 0.2 all-gather.2.cloned.1.call-start
  154.6 3.1 reshape.199
  157.8 0.2 convert_reduce_fusion
  158.1 6.0 %gather_fusion.1 = bf16[32,128,640]{2,1,0:T(8,128)(2,1)} fusion(bf16[32,128,640]{2,1,0:T(8,128)(2,1)} %bitcast.53, s32[1024]{0:T(1024)S(1)} %pad_clamp_fusion), kind=kCustom, calls=%fused_computation.1.clone | custom fusion | bytes 10485888 | tf_op jit(solution)/shard_map/jit(_take)/gather | solution.py:50
  164.1 104.8 %all-to-all-done.1 = bf16[8,4,128,640]{3,2,1,0:T(8,128)(2,1)} async-done(((bf16[8,4,128,640]{3,2,1,0:T(8,128)(2,1)}), bf16[8,4,128,640]{3,2,1,0:T(8,128)(2,1)}, u32[]{:S(2)}, u32[]{:S(2)}) %all-to-all-start.1) | async-done | bytes 5242912 | tf_op jit(solution)/shard_map/all_to_all | solution.py:38
  268.9 6.0 %gather_fusion.3 = bf16[32,128,640]{2,1,0:T(8,128)(2,1)} fusion(bf16[32,128,640]{2,1,0:T(8,128)(2,1)} %bitcast.10, s32[1024]{0:T(1024)S(1)} %pad_clamp_fusion), kind=kCustom, calls=%fused_computation.3.clone | custom fusion | bytes 10485888 | tf_op jit(solution)/shard_map/jit(_take)/gather | solution.py:49
  274.9 9.1 %broadcast_select_fusion.1 = (bf16[32,128,640]{2,1,0:T(8,128)(2,1)}, bf16[32,128,640]{2,1,0:T(8,128)(2,1)}) fusion(bf16[32,128,640]{2,1,0:T(8,128)(2,1)} %gather_fusion.1, pred[32]{0:T(512)(128)(4,1)S(1)} %get-tuple-element.6, bf16[32,128,640]{2,1,0:T(8,128)(2,1)} %gather_fusion.3), kind=kLoop, calls=%fused_computation.21 | loop fusion | flops 5242880 | bytes 20971552 | tf_op jit(solution)/shard_map/jit(_take)/select_n | solution.py:50
  284.1 5.9 %pad_maximum_fusion.1 = bf16[8,5,128,640]{3,2,1,0:T(8,128)(2,1)} fusion(bf16[8,4,128,640]{3,2,1,0:T(8,128)(2,1)} %bitcast.55, bf16[8,1,128,640]{3,2,1,0:T(8,128)(2,1)S(1)} %bitcast.48), kind=kLoop, calls=%fused_computation.12 | loop fusion | flops 3276800 | bytes 13107200 | tf_op jit(solution)/shard_map/concatenate | solution.py:55
  289.9 15.2 %reshape.152 = bf16[8,640,5,128]{3,2,1,0:T(8,128)(2,1)} reshape(bf16[8,5,128,640]{3,2,1,0:T(8,128)(2,1)} %pad_maximum_fusion.1) | data formatting | bytes 13107200 | tf_op jit(solution)/shard_map/reshape | solution.py:55
  305.1 5.9 %pad_maximum_fusion = bf16[8,5,128,640]{3,2,1,0:T(8,128)(2,1)} fusion(bf16[8,4,128,640]{3,2,1,0:T(8,128)(2,1)} %bitcast.54, bf16[8,1,128,640]{3,2,1,0:T(8,128)(2,1)S(1)} %bitcast.50), kind=kLoop, calls=%fused_computation.11 | loop fusion | flops 3276800 | bytes 13107200 | tf_op jit(solution)/shard_map/concatenate | solution.py:58
  311.0 15.1 %reshape.147 = bf16[8,640,5,128]{3,2,1,0:T(8,128)(2,1)} reshape(bf16[8,5,128,640]{3,2,1,0:T(8,128)(2,1)} %pad_maximum_fusion) | data formatting | bytes 13107200 | tf_op jit(solution)/shard_map/reshape | solution.py:58
  326.1 6.3 %bitcast_reduce_fusion = (f32[8,5,128]{2,1,0:T(8,128)S(1)}, f32[8,5,640,128]{3,2,1,0:T(8,128)S(1)}) fusion(pred[8,640]{1,0:T(8,128)(4,1)S(1)} %broadcast_bitcast_fusion, bf16[8,128,5,128]{3,2,1,0:T(8,128)(2,1)S(1)} %reshape.199, bf16[8,640,5,128]{3,2,1,0:T(8,128)(2,1)} %reshape.152), kind=kOutput, calls=%fused_computation.5 | convolution fusion | flops 848686080 | bytes 20997120 | tf_op jit(solution)/shard_map/bqhd,bkhd->bhqk/dot_general | solution.py:63
  332.4 3.0 fusion.1
  335.4 8.2 %fusion.12 = bf16[8,128,5,128]{1,3,2,0:T(8,128)(2,1)S(1)} fusion(f32[8,5,640,128]{3,2,1,0:T(8,128)S(1)} %get-tuple-element.14, f32[8,5,128]{2,1,0:T(8,128)S(1)} %get-tuple-element.13, pred[8,640]{1,0:T(8,128)(4,1)S(1)} %broadcast_bitcast_fusion, bf16[8,640,5,128]{3,2,1,0:T(8,128)(2,1)} %reshape.147, f32[8,128,5]{1,2,0:T(8,128)S(1)} %bitcast.61), kind=kOutput, calls=%fused_computation.26 | convolution fusion | flops 853278720 | bytes 21017600 | tf_op jit(solution)/shard_map/bhqk,bkhd->bqhd/dot_general | solution.py:75
  343.6 0.9 copy.45
  344.5 1.4 copy.65
  345.9 9.7 %copy.46 = bf16[640,5120]{0,1:T(8,128)(2,1)} copy(bf16[640,5120]{1,0:T(8,128)(2,1)} %param.15) | data formatting | bytes 13107200 | tf_op args[5]
  355.7 98.6 %all_to_all.30 = bf16[640,4,1280]{0,2,1:T(8,128)(2,1)} all-to-all(bf16[640,4,1280]{0,2,1:T(8,128)(2,1)} %bitcast.52), channel_id=1, replica_groups=mesh['frames'=8,'heads'=4] {'heads'}, dimensions={1} | all-to-all | bytes 13107200 | tf_op jit(solution)/shard_map/all_to_all | solution.py:78
  454.2 9.5 %copy.47 = bf16[4,640,1280]{2,1,0:T(8,128)(2,1)} copy(bf16[4,640,1280]{1,2,0:T(8,128)(2,1)} %bitcast.51) | data formatting | bytes 13107200 | tf_op jit(solution)/shard_map/all_to_all | solution.py:78
  463.7 12.0 %convolution_convert_fusion = bf16[1024,1280]{1,0:T(8,128)(2,1)} fusion(bf16[1024,2560]{0,1:T(8,128)(2,1)} %all-gather.2.cloned.1.call-done, bf16[2560,1280]{1,0:T(8,128)(2,1)} %bitcast.58), kind=kOutput, calls=%fused_computation.24 | convolution fusion | flops 6712197120 | bytes 14417920 | tf_op jit(solution)/shard_map/dot_general | solution.py:79
  (27 shorter events, 0.7 us)
Async XLA Ops:
  8.9 4.9 %copy-start = (bf16[1024,640]{1,0:T(8,128)(2,1)S(1)}, bf16[1024,640]{1,0:T(8,128)(2,1)}, u32[]{:S(2)}) copy-start(bf16[1024,640]{1,0:T(8,128)(2,1)} %param.11) | copy-start | bytes 3932164
  149.4 5.0 %copy-start.2 = (s32[64,4]{0,1:T(4,128)S(1)}, s32[64,4]{0,1:T(4,128)}, u32[]{:S(2)}) copy-start(s32[64,4]{0,1:T(4,128)} %param.13) | copy-start | bytes 3076
  149.4 8.4 %copy-start.3 = (s32[8]{0:T(128)S(1)}, s32[8]{0:T(128)}, u32[]{:S(2)}) copy-start(s32[8]{0:T(128)} %param.14) | copy-start | bytes 100
  149.4 119.5 %all-to-all-start.1 = ((bf16[8,4,128,640]{3,2,1,0:T(8,128)(2,1)}), bf16[8,4,128,640]{3,2,1,0:T(8,128)(2,1)}, u32[]{:S(2)}, u32[]{:S(2)}) async-start(bf16[8,4,128,640]{3,2,1,0:T(8,128)(2,1)} %bitcast.56), calls=%async_computation.1 | async-start | bytes 10485760 | tf_op jit(solution)/shard_map/all_to_all | solution.py:38
  154.2 309.6 %all-gather.2.cloned.1.call-start = ((), (), s32[]{:S(2)}) async-start(), calls=%async_computation.3 | async-start | bytes 6553600 | tf_op jit(solution)/shard_map/all_gather | solution.py:80
  289.9 15.2 %copy-start.1 = (bf16[1024,640]{1,0:T(8,128)(2,1)S(1)}, bf16[1024,640]{1,0:T(8,128)(2,1)}, u32[]{:S(2)}) copy-start(bf16[1024,640]{1,0:T(8,128)(2,1)} %param.12) | copy-start | bytes 3932164
Sparse Core Ops, SparseCore 0:
  346.0 57.8 all-gather.1
where the time goes:
time: 484 us; the launch traced here: 483 us
  blocking collectives  222 us (46%)
  waiting for transfers between devices  105 us (22%)
  local copies, waits for them, and re-layouts  76.1 us (16%)
  other arithmetic  35 us (7%)
  matrix products  26.5 us (5%)
  between operations  13.5 us (3%)
  starting transfers between devices  5 us (1%)
    all_to_all x1, blocking collectives, shards(): lax.all_to_all(send_values, 'frames', split_axis=0, concat_axis=0, tiled=...  123 us
    all_to_all x1, waiting for transfers between devices, shards(): lax.all_to_all(send_keys, 'frames', split_axis=0, concat_axis=0, tiled=True)  105 us
    all_to_all x1, blocking collectives, shards(): lax.all_to_all(w_out, 'heads', split_axis=1, concat_axis=0, tiled=True)  98.6 us
    reshape x1, local copies, waits for them, and re-layouts, shards(): jnp.concatenate([key_tiles[:, None], chosen_keys], 1)  15.2 us
    reshape x1, local copies, waits for them, and re-layouts, shards(): jnp.concatenate([value_tiles[:, None], chosen_values], 1)  15.1 us
    dot_general x1, matrix products, shards(): jnp.dot(lax.all_gather(attn, 'heads', axis=1, tiled=True), all_rows, pref...  12 us
    unnamed x10, local copies, waits for them, and re-layouts  11.2 us
  transfers between devices with their start and end apart: 2, of which 1 were waited for; matrix products, arithmetic and copies ran while one was open for 6% of the time, Pallas kernels for 0%

commit v1 on v0

v1 whole, which is shorter than its diff:
```python
import functools

import jax
import jax.numpy as jnp
from jax import lax
from jax.experimental import pallas as pl
from jax.experimental.pallas import tpu as pltpu
from jax.sharding import PartitionSpec as P

DH = 128
TILE = 128
MESH = pl.DeviceIdType.MESH
F32 = jnp.float32
NT_DIMS = (((1,), (1,)), ((), ()))


def layer_kernel(
    dims, pick_ref, slot_ref, count_ref, q_ref, k_ref, v_ref, w_ref, out_ref,
    send, rows, attn, acc, kv_send, kv_recv, w_send, w_recv, a_send, a_recv, own_sem, *recv,
):
    frames, peers, blocks, select, capacity, heads, slots = dims
    me_f, me_p = lax.axis_index("frames"), lax.axis_index("heads")
    depth = heads * DH
    features = rows.shape[2]

    barrier = pltpu.get_barrier_semaphore()

    @pl.loop(1, frames)
    def _(step):
        pl.semaphore_signal(
            barrier, inc=1, device_id=(lax.rem(me_f + step, frames), me_p), device_id_type=MESH
        )

    @pl.loop(1, peers)
    def _(step):
        pl.semaphore_signal(
            barrier, inc=1, device_id=(me_f, lax.rem(me_p + step, peers)), device_id_type=MESH
        )

    def columns_of(peer):
        return pl.ds(pl.multiple_of(peer * features, features), features)

    own_rows = pltpu.make_async_copy(w_ref.at[:, columns_of(me_p)], rows.at[me_p], own_sem)
    own_rows.start()

    def head_columns(h):
        return slice(h * DH, (h + 1) * DH)

    def kv_copy(h, target, origin):
        return pltpu.make_async_remote_copy(
            src_ref=send.at[h % slots, target],
            dst_ref=recv[h].at[pl.ds(origin * capacity, capacity)],
            send_sem=kv_send.at[h, target],
            recv_sem=kv_recv.at[h, origin],
            device_id=(target, me_p),
            device_id_type=MESH,
        )

    def build_kv(h):
        if h >= slots:

            @pl.loop(1, frames)
            def _(step):
                kv_copy(h - slots, lax.rem(me_f + step, frames), me_f).wait_send()

        @pl.loop(1, frames)
        def _(step):
            target = lax.rem(me_f + step, frames)
            for c in range(capacity):
                index = pick_ref[target * capacity + c]
                send[h % slots, target, c, 0] = k_ref[index, :, head_columns(h)]
                send[h % slots, target, c, 1] = v_ref[index, :, head_columns(h)]

        for c in range(capacity):
            index = pick_ref[me_f * capacity + c]
            recv[h][me_f * capacity + c, 0] = k_ref[index, :, head_columns(h)]
            recv[h][me_f * capacity + c, 1] = v_ref[index, :, head_columns(h)]

    def start_kv(h):
        @pl.loop(1, frames)
        def _(step):
            kv_copy(h, lax.rem(me_f + step, frames), me_f).start()

    def wait_kv(h):
        @pl.loop(1, frames)
        def _(step):
            origin = lax.rem(me_f + step, frames)
            kv_copy(h, origin, origin).wait_recv()

    def w_copy(target, origin):
        return pltpu.make_async_remote_copy(
            src_ref=w_ref.at[:, columns_of(target)],
            dst_ref=rows.at[origin],
            send_sem=w_send.at[target],
            recv_sem=w_recv.at[origin],
            device_id=(me_f, target),
            device_id_type=MESH,
        )

    def a_copy(h, target, origin):
        return pltpu.make_async_remote_copy(
            src_ref=attn.at[h, me_p],
            dst_ref=attn.at[h, origin],
            send_sem=a_send.at[h, target],
            recv_sem=a_recv.at[h, origin],
            device_id=(me_f, target),
            device_id_type=MESH,
        )

    def over_peers(action):
        @pl.loop(1, peers)
        def _(step):
            action(lax.rem(me_p + step, peers))

    def attend(h):
        @pl.loop(0, blocks)
        def _(b):
            q = q_ref[b, :, head_columns(h)]
            picks = [slot_ref[b * select + s] for s in range(select)]
            keyset = jnp.concatenate(
                [k_ref[b, :, head_columns(h)]] + [recv[h][i, 0] for i in picks], axis=0
            )
            valueset = jnp.concatenate(
                [v_ref[b, :, head_columns(h)]] + [recv[h][i, 1] for i in picks], axis=0
            )
            scores = lax.dot_general(q, keyset, NT_DIMS, preferred_element_type=F32)
            scores = scores * (1.0 / DH**0.5)
            position = lax.broadcasted_iota(jnp.int32, scores.shape, 1)
            scores = jnp.where(position < (count_ref[b] + 1) * TILE, scores, -jnp.inf)
            top = jnp.max(scores, axis=1, keepdims=True)
            probs = jnp.exp(scores - top)
            denom = jnp.sum(probs, axis=1, keepdims=True)
            mixed = jnp.dot(probs.astype(jnp.bfloat16), valueset, preferred_element_type=F32)
            attn[h, me_p, pl.ds(pl.multiple_of(b * TILE, TILE), TILE), :] = (mixed / denom).astype(
                jnp.bfloat16
            )

    row_tile = 2 * TILE

    def project(h):
        @pl.loop(0, blocks * TILE // row_tile)
        def _(r):
            span = pl.ds(pl.multiple_of(r * row_tile, row_tile), row_tile)
            left = jnp.concatenate([attn[h, p, span, :] for p in range(peers)], axis=1)
            right = jnp.concatenate([rows[p, head_columns(h), :] for p in range(peers)], axis=0)
            term = jnp.dot(left, right, preferred_element_type=F32)
            if h > 0:
                term = term + acc[span, :]
            if h == heads - 1:
                out_ref[span, :] = term.astype(out_ref.dtype)
            else:
                acc[span, :] = term

    build_kv(0)
    pl.semaphore_wait(barrier, frames + peers - 2)
    start_kv(0)
    over_peers(lambda target: w_copy(target, me_p).start())
    if heads > 1:
        build_kv(1)
        start_kv(1)
    for h in range(heads):
        if h + 2 < heads:
            build_kv(h + 2)
        wait_kv(h)
        if h + 2 < heads:
            start_kv(h + 2)
        attend(h)
        over_peers(lambda target: a_copy(h, target, me_p).start())
        if h == 0:
            own_rows.wait()
            over_peers(lambda origin: w_copy(origin, origin).wait_recv())
        else:
            over_peers(lambda origin: a_copy(h - 1, origin, origin).wait_recv())
            project(h - 1)
    over_peers(lambda origin: a_copy(heads - 1, origin, origin).wait_recv())
    project(heads - 1)
    for h in range(max(0, heads - slots), heads):

        @pl.loop(1, frames)
        def _(step):
            kv_copy(h, lax.rem(me_f + step, frames), me_f).wait_send()

    over_peers(lambda target: w_copy(target, me_p).wait_send())
    for h in range(heads):
        over_peers(lambda target: a_copy(h, target, me_p).wait_send())


def shards(queries, keys, values, block_ids, counts, w_out):
    frames = lax.axis_size("frames")
    peers = lax.axis_size("heads")
    here = lax.axis_index("frames")
    tokens, width = queries.shape
    blocks = tokens // TILE
    select = block_ids.shape[1]
    heads = width // DH
    requests = blocks * select
    capacity = max(2, (requests + frames - 1) // frames)
    features = w_out.shape[1] // peers
    slots = min(3, heads)

    ids = block_ids.reshape(frames, requests)
    owner = ids // blocks
    local = ids % blocks
    mine = owner == here
    order = jnp.arange(requests, dtype=jnp.int32)
    before = order[:, None] < order[None, :]
    rank = jnp.sum((mine[:, :, None] & before[None]).astype(jnp.int32), axis=1)
    hit = mine[:, :, None] & (rank[:, :, None] == jnp.arange(capacity, dtype=jnp.int32))
    pick = jnp.sum(jnp.where(hit, local[:, :, None], 0), axis=1).reshape(-1)
    my_owner = lax.dynamic_slice_in_dim(owner, here, 1, 0).reshape(requests)
    same = (my_owner[:, None] == my_owner[None, :]) & before
    my_slot = my_owner * capacity + jnp.sum(same.astype(jnp.int32), axis=0)

    smem = pl.BlockSpec(memory_space=pltpu.SMEM)
    vmem = pl.BlockSpec(memory_space=pltpu.VMEM)
    tiles = (blocks, TILE, width)
    dma = pltpu.SemaphoreType.DMA
    return pl.pallas_call(
        functools.partial(layer_kernel, (frames, peers, blocks, select, capacity, heads, slots)),
        out_shape=jax.ShapeDtypeStruct((tokens, features), jnp.bfloat16),
        in_specs=[smem, smem, smem, vmem, vmem, vmem, pl.BlockSpec(memory_space=pl.ANY)],
        out_specs=vmem,
        scratch_shapes=[
            pltpu.VMEM((slots, frames, capacity, 2, TILE, DH), jnp.bfloat16),
            pltpu.VMEM((peers, width, features), jnp.bfloat16),
            pltpu.VMEM((heads, peers, tokens, DH), jnp.bfloat16),
            pltpu.VMEM((tokens, features), F32),
            dma((heads, frames)),
            dma((heads, frames)),
            dma((peers,)),
            dma((peers,)),
            dma((heads, peers)),
            dma((heads, peers)),
            dma,
        ]
        + [pltpu.VMEM((frames * capacity, 2, TILE, DH), jnp.bfloat16)] * heads,
        compiler_params=pltpu.CompilerParams(
            collective_id=0, has_side_effects=True, vmem_limit_bytes=67043328
        ),
    )(
        pick, my_slot, counts, queries.reshape(tiles), keys.reshape(tiles), values.reshape(tiles),
        w_out,
    )


def solution(mesh):
    placed = (
        P("frames", "heads"),
        P("frames", "heads"),
        P("frames", "heads"),
        P(),
        P("frames"),
        P("heads", None),
    )
    return jax.shard_map(
        shards, mesh=mesh, in_specs=placed, out_specs=P("frames", "heads"), check_vma=False
    )
```

time: 484 us -> 263 us (0.54)
  the two profiles are of different devices: /device:TPU:0 before, /device:TPU:15 now
where the time goes in v1:
time: 263 us; the launch traced here: 262 us
  Pallas kernels  257 us (98%)
  local copies, waits for them, and re-layouts  4.94 us (2%)
    pallas_call x1, Pallas kernels, shards(): pl.pallas_call(functools.partial(layer_kernel, (frames, peers, blocks, se...  257 us

profile of v1, /device:TPU:15, one launch (start us, length us, event | category | flops | bytes accessed | tf_op | source)
XLA Modules:
  0.0 262.4 jit_solution(12738190256435203464)
XLA Ops:
  0.0 0.8 copy.8
  0.8 0.1 reshape.82
  0.9 0.1 convert_reduce_fusion
  1.0 0.1 select_reduce_fusion
  1.2 0.1 convert_reduce_fusion.1
  1.3 0.5 multiply_add_fusion.slot_ref
  1.8 0.1 copy.9
  1.9 0.6 reshape.83.pick_ref
  2.5 256.5 %shard_map.64 = bf16[1024,1280]{1,0:T(8,128)(2,1)} custom-call(s32[32]{0:T(128)} %reshape.83.pick_ref, s32[32]{0:T(128)} %multiply_add_fusion.slot_ref, s32[8]{0:T(128)} %count_ref.1, bf16[8,128,640]{2,1,0:T(8,128)(2,1)} %bitcast.7, bf16[8,128,640]{2,1,0:T(8,128)(2,1)} %bitcast.8, bf16[8,128,640]{2,1,0:T(8,128)(2,1)} %bitcast.9, bf16[640,5120]{1,0:T(8,128)(2,1)} %w_ref.1), custom_call_target="tpu_custom_call" | custom-call | tf_op jit(solution)/shard_map/pallas_call | solution.py:218
  259.0 3.4 %copy.11 = bf16[1024,1280]{1,0:T(8,128)(2,1)} copy(bf16[1024,1280]{1,0:T(8,128)(2,1)} %shard_map.64) | data formatting | bytes 5242880
  (4 shorter events, 0.0 us)

commit v2 on v1

--- a/solution.py
+++ b/solution.py
@@ -1,4 +1,5 @@
 import functools
+import math
 
 import jax
 import jax.numpy as jnp
@@ -11,14 +12,216 @@
 TILE = 128
 MESH = pl.DeviceIdType.MESH
 F32 = jnp.float32
+PAIR = 2
+AHEAD = 2
+VMEM_BYTES = 67043328
 NT_DIMS = (((1,), (1,)), ((), ()))
 
 
+def head_columns(h):
+    return slice(h * DH, (h + 1) * DH)
+
+
+class direct_exchange:
+    def __init__(self, dims, pick_ref, k_ref, v_ref, recv, send, kv_send, kv_recv):
+        self.frames, _, _, _, self.capacity, self.heads, self.slots = dims
+        self.pick_ref, self.k_ref, self.v_ref, self.recv = pick_ref, k_ref, v_ref, recv
+        self.send, self.kv_send, self.kv_recv = send, kv_send, kv_recv
+        self.me_f, self.me_p = lax.axis_index("frames"), lax.axis_index("heads")
+
+    def copy(self, h, target, origin):
+        return pltpu.make_async_remote_copy(
+            src_ref=self.send.at[h % self.slots, target],
+            dst_ref=self.recv[h].at[pl.ds(origin * self.capacity, self.capacity)],
+            send_sem=self.kv_send.at[h, target],
+            recv_sem=self.kv_recv.at[h, origin],
+            device_id=(target, self.me_p),
+            device_id_type=MESH,
+        )
+
+    def others(self, action):
+        @pl.loop(1, self.frames)
+        def _(step):
+            action(lax.rem(self.me_f + step, self.frames))
+
+    def pick(self, target, c):
+        return self.pick_ref[(target * self.frames + self.me_f) * self.capacity + c]
+
+    def build(self, h):
+        if h >= self.slots:
+            self.others(lambda target: self.copy(h - self.slots, target, self.me_f).wait_send())
+
+        def fill(target):
+            for c in range(self.capacity):
+                index = self.pick(target, c)
+                self.send[h % self.slots, target, c, 0] = self.k_ref[index, :, head_columns(h)]
+                self.send[h % self.slots, target, c, 1] = self.v_ref[index, :, head_columns(h)]
+
+        self.others(fill)
+        for c in range(self.capacity):
+            index = self.pick(self.me_f, c)
+            self.recv[h][self.me_f * self.capacity + c, 0] = self.k_ref[index, :, head_columns(h)]
+            self.recv[h][self.me_f * self.capacity + c, 1] = self.v_ref[index, :, head_columns(h)]
+
+    def start(self, h):
+        self.others(lambda target: self.copy(h, target, self.me_f).start())
+
+    def prepare(self):
+        self.build(0)
+
+    def begin(self):
+        self.start(0)
+
+    def follow(self):
+        if self.heads > 1:
+            self.build(1)
+            self.start(1)
+
+    def receive(self, h):
+        if h + 2 < self.heads:
+            self.build(h + 2)
+        self.others(lambda origin: self.copy(h, origin, origin).wait_recv())
+        if h + 2 < self.heads:
+            self.start(h + 2)
+
+    def drain(self):
+        for h in range(max(0, self.heads - self.slots), self.heads):
+            self.others(lambda target: self.copy(h, target, self.me_f).wait_send())
+
+
+class relay_exchange:
+    def __init__(
+        self, dims, pick_ref, k_ref, v_ref, recv,
+        picked, up_send, up_recv, down_send, down_recv, x_send, x_recv, *passing,
+    ):
+        self.frames, _, self.blocks, _, self.capacity, self.heads, _ = dims
+        self.line = self.frames // PAIR
+        self.pick_ref, self.k_ref, self.v_ref, self.recv = pick_ref, k_ref, v_ref, recv
+        self.picked, self.x_send, self.x_recv = picked, x_send, x_recv
+        self.sems = ((up_send, up_recv), (down_send, down_recv))
+        self.passing = passing
+        self.me_f, self.me_p = lax.axis_index("frames"), lax.axis_index("heads")
+        self.z, self.x = self.me_f // PAIR, self.me_f % PAIR
+        self.partner = self.z * PAIR + (PAIR - 1 - self.x)
+
+    def held(self, h, way, far):
+        return self.passing[(h * 2 + way) * (self.line - 1) + far - 1]
+
+    def at(self, way, steps):
+        return self.z + steps if way == 0 else self.z - steps
+
+    def inside(self, position):
+        return (position >= 0) & (position < self.line)
+
+    def onward(self, h, way, far, kv):
+        source = (self.k_ref, self.v_ref)[kv].at[:, :, head_columns(h)]
+        if far > 0:
+            source = self.held(h, way, far).at[kv]
+        send_sem, recv_sem = self.sems[way]
+        return pltpu.make_async_remote_copy(
+            src_ref=source,
+            dst_ref=self.held(h, way, far + 1).at[kv],
+            send_sem=send_sem.at[h, far, kv],
+            recv_sem=recv_sem.at[h, far, kv],
+            device_id=(self.at(way, 1) * PAIR + self.x, self.me_p),
+            device_id_type=MESH,
+        )
+
+    def beside(self, h, origin_z, column):
+        return pltpu.make_async_remote_copy(
+            src_ref=self.picked.at[h, origin_z],
+            dst_ref=self.recv[h].at[
+                pl.ds((origin_z * PAIR + column) * self.capacity, self.capacity)
+            ],
+            send_sem=self.x_send.at[h, origin_z],
+            recv_sem=self.x_recv.at[h, origin_z],
+            device_id=(self.partner, self.me_p),
+            device_id_type=MESH,
+        )
+
+    def send_on(self, h, way, far):
+        @pl.when(self.inside(self.at(way, 1)))
+        def _():
+            for kv in range(2):
+                self.onward(h, way, far, kv).start()
+
+    def hand_out(self, h, origin_z, load):
+        origin = origin_z * PAIR + self.x
+        for c in range(self.capacity):
+            theirs = self.pick_ref[(self.partner * self.frames + origin) * self.capacity + c]
+            for kv in range(2):
+                self.picked[h, origin_z, c, kv] = load(kv, theirs)
+        for c in range(self.capacity):
+            ours = self.pick_ref[(self.me_f * self.frames + origin) * self.capacity + c]
+            for kv in range(2):
+                self.recv[h][origin * self.capacity + c, kv] = load(kv, ours)
+        self.beside(h, origin_z, self.x).start()
+
+    def own(self, h):
+        def load(kv, index):
+            return (self.k_ref, self.v_ref)[kv][index, :, head_columns(h)]
+
+        self.hand_out(h, self.z, load)
+
+    def arrive(self, h, far):
+        for way in range(2):
+            @pl.when(self.inside(self.at(way, -far)))
+            def _():
+                for kv in range(2):
+                    self.onward(h, way, far - 1, kv).wait_recv()
+                if far + 1 < self.line:
+                    self.send_on(h, way, far)
+
+        for way in range(2):
+            @pl.when(self.inside(self.at(way, -far)))
+            def _():
+                held = self.held(h, way, far)
+                self.hand_out(h, self.at(way, -far), lambda kv, index: held[kv, index])
+
+    def prepare(self):
+        pass
+
+    def begin(self):
+        for h in range(min(AHEAD, self.heads)):
+            for way in range(2):
+                self.send_on(h, way, 0)
+
+    def follow(self):
+        self.own(0)
+
+    def receive(self, h):
+        for far in range(1, self.line):
+            self.arrive(h, far)
+            if far == 1 and h + AHEAD < self.heads:
+                for way in range(2):
+                    self.send_on(h + AHEAD, way, 0)
+        if h + 1 < self.heads:
+            self.own(h + 1)
+
+        @pl.loop(0, self.line)
+        def _(origin_z):
+            self.beside(h, origin_z, PAIR - 1 - self.x).wait_recv()
+
+    def drain(self):
+        for h in range(self.heads):
+            for way in range(2):
+                for far in range(self.line - 1):
+                    @pl.when(self.inside(self.at(way, -far)) & self.inside(self.at(way, 1)))
+                    def _():
+                        for kv in range(2):
+                            self.onward(h, way, far, kv).wait_send()
+
+            @pl.loop(0, self.line)
+            def _(origin_z):
+                self.beside(h, origin_z, self.x).wait_send()
+
+
 def layer_kernel(
-    dims, pick_ref, slot_ref, count_ref, q_ref, k_ref, v_ref, w_ref, out_ref,
-    send, rows, attn, acc, kv_send, kv_recv, w_send, w_recv, a_send, a_recv, own_sem, *recv,
+    dims, relayed, pick_ref, slot_ref, count_ref, q_ref, k_ref, v_ref, w_ref, out_ref,
+    rows, attn, acc, w_send, w_recv, a_send, a_recv, own_sem, *kv_refs,
 ):
     frames, peers, blocks, select, capacity, heads, slots = dims
+    recv, kv_refs = kv_refs[:heads], kv_refs[heads:]
     me_f, me_p = lax.axis_index("frames"), lax.axis_index("heads")
     depth = heads * DH
     features = rows.shape[2]
@@ -43,49 +246,9 @@
     own_rows = pltpu.make_async_copy(w_ref.at[:, columns_of(me_p)], rows.at[me_p], own_sem)
     own_rows.start()
 
-    def head_columns(h):
-        return slice(h * DH, (h + 1) * DH)
-
-    def kv_copy(h, target, origin):
-        return pltpu.make_async_remote_copy(
-            src_ref=send.at[h % slots, target],
-            dst_ref=recv[h].at[pl.ds(origin * capacity, capacity)],
-            send_sem=kv_send.at[h, target],
-            recv_sem=kv_recv.at[h, origin],
-            device_id=(target, me_p),
-            device_id_type=MESH,
-        )
-
-    def build_kv(h):
-        if h >= slots:
-
-            @pl.loop(1, frames)
-            def _(step):
-                kv_copy(h - slots, lax.rem(me_f + step, frames), me_f).wait_send()
-
-        @pl.loop(1, frames)
-        def _(step):
-            target = lax.rem(me_f + step, frames)
-            for c in range(capacity):
-                index = pick_ref[target * capacity + c]
-                send[h % slots, target, c, 0] = k_ref[index, :, head_columns(h)]
-                send[h % slots, target, c, 1] = v_ref[index, :, head_columns(h)]
-
-        for c in range(capacity):
-            index = pick_ref[me_f * capacity + c]
-            recv[h][me_f * capacity + c, 0] = k_ref[index, :, head_columns(h)]
-            recv[h][me_f * capacity + c, 1] = v_ref[index, :, head_columns(h)]
-
-    def start_kv(h):
-        @pl.loop(1, frames)
-        def _(step):
-            kv_copy(h, lax.rem(me_f + step, frames), me_f).start()
-
-    def wait_kv(h):
-        @pl.loop(1, frames)
-        def _(step):
-            origin = lax.rem(me_f + step, frames)
-            kv_copy(h, origin, origin).wait_recv()
+    exchange = (relay_exchange if relayed else direct_exchange)(
+        dims, pick_ref, k_ref, v_ref, recv, *kv_refs
+    )
 
     def w_copy(target, origin):
         return pltpu.make_async_remote_copy(
@@ -151,19 +314,13 @@
             else:
                 acc[span, :] = term
 
-    build_kv(0)
+    exchange.prepare()
     pl.semaphore_wait(barrier, frames + peers - 2)
-    start_kv(0)
+    exchange.begin()
     over_peers(lambda target: w_copy(target, me_p).start())
-    if heads > 1:
-        build_kv(1)
-        start_kv(1)
+    exchange.follow()
     for h in range(heads):
-        if h + 2 < heads:
-            build_kv(h + 2)
-        wait_kv(h)
-        if h + 2 < heads:
-            start_kv(h + 2)
+        exchange.receive(h)
         attend(h)
         over_peers(lambda target: a_copy(h, target, me_p).start())
         if h == 0:
@@ -174,12 +331,7 @@
             project(h - 1)
     over_peers(lambda origin: a_copy(heads - 1, origin, origin).wait_recv())
     project(heads - 1)
-    for h in range(max(0, heads - slots), heads):
-
-        @pl.loop(1, frames)
-        def _(step):
-            kv_copy(h, lax.rem(me_f + step, frames), me_f).wait_send()
-
+    exchange.drain()
     over_peers(lambda target: w_copy(target, me_p).wait_send())
     for h in range(heads):
         over_peers(lambda target: a_copy(h, target, me_p).wait_send())
@@ -200,42 +352,53 @@
 
     ids = block_ids.reshape(frames, requests)
     owner = ids // blocks
-    local = ids % blocks
-    mine = owner == here
     order = jnp.arange(requests, dtype=jnp.int32)
-    before = order[:, None] < order[None, :]
-    rank = jnp.sum((mine[:, :, None] & before[None]).astype(jnp.int32), axis=1)
-    hit = mine[:, :, None] & (rank[:, :, None] == jnp.arange(capacity, dtype=jnp.int32))
-    pick = jnp.sum(jnp.where(hit, local[:, :, None], 0), axis=1).reshape(-1)
-    my_owner = lax.dynamic_slice_in_dim(owner, here, 1, 0).reshape(requests)
-    same = (my_owner[:, None] == my_owner[None, :]) & before
-    my_slot = my_owner * capacity + jnp.sum(same.astype(jnp.int32), axis=0)
+    same = (owner[:, :, None] == owner[:, None, :]) & (order[:, None] < order[None, :])
+    slot = owner * capacity + jnp.sum(same.astype(jnp.int32), axis=1)
+    hit = slot[:, None, :] == jnp.arange(frames * capacity, dtype=jnp.int32)[:, None]
+    pick = jnp.sum(jnp.where(hit, (ids % blocks)[:, None, :], 0), axis=2).reshape(-1)
+    my_slot = lax.dynamic_slice_in_dim(slot, here, 1, 0).reshape(requests)
 
     smem = pl.BlockSpec(memory_space=pltpu.SMEM)
     vmem = pl.BlockSpec(memory_space=pltpu.VMEM)
     tiles = (blocks, TILE, width)
     dma = pltpu.SemaphoreType.DMA
+    bf16 = jnp.bfloat16
+    line = frames // PAIR
+    common = [
+        pltpu.VMEM((peers, width, features), bf16),
+        pltpu.VMEM((heads, peers, tokens, DH), bf16),
+        pltpu.VMEM((tokens, features), F32),
+    ]
+    common_sems = [
+        dma((peers,)), dma((peers,)), dma((heads, peers)), dma((heads, peers)), dma,
+    ]
+    recv = [pltpu.VMEM((frames * capacity, 2, TILE, DH), bf16)] * heads
+    picked = pltpu.VMEM((heads, line, capacity, 2, TILE, DH), bf16)
+    passing = [pltpu.VMEM((2, blocks, TILE, DH), bf16)] * (heads * 2 * (line - 1))
+    operands = tokens * (3 * width + features) * 2
+    needed = operands + sum(
+        math.prod(m.shape) * jnp.dtype(m.dtype).itemsize
+        for m in common + recv + [picked] + passing
+    )
+    relayed = frames % PAIR == 0 and needed < VMEM_BYTES * 15 // 16
+    if relayed:
+        extra = [picked] + [dma((heads, line, 2))] * 4 + [dma((heads, line))] * 2 + passing
+    else:
+        extra = [
+            pltpu.VMEM((slots, frames, capacity, 2, TILE, DH), bf16),
+            dma((heads, frames)),
+            dma((heads, frames)),
+        ]
+    dims = (frames, peers, blocks, select, capacity, heads, slots)
     return pl.pallas_call(
-        functools.partial(layer_kernel, (frames, peers, blocks, select, capacity, heads, slots)),
-        out_shape=jax.ShapeDtypeStruct((tokens, features), jnp.bfloat16),
+        functools.partial(layer_kernel, dims, relayed),
+        out_shape=jax.ShapeDtypeStruct((tokens, features), bf16),
         in_specs=[smem, smem, smem, vmem, vmem, vmem, pl.BlockSpec(memory_space=pl.ANY)],
         out_specs=vmem,
-        scratch_shapes=[
-            pltpu.VMEM((slots, frames, capacity, 2, TILE, DH), jnp.bfloat16),
-            pltpu.VMEM((peers, width, features), jnp.bfloat16),
-            pltpu.VMEM((heads, peers, tokens, DH), jnp.bfloat16),
-            pltpu.VMEM((tokens, features), F32),
-            dma((heads, frames)),
-            dma((heads, frames)),
-            dma((peers,)),
-            dma((peers,)),
-            dma((heads, peers)),
-            dma((heads, peers)),
-            dma,
-        ]
-        + [pltpu.VMEM((frames * capacity, 2, TILE, DH), jnp.bfloat16)] * heads,
+        scratch_shapes=common + common_sems + recv + extra,
         compiler_params=pltpu.CompilerParams(
-            collective_id=0, has_side_effects=True, vmem_limit_bytes=67043328
+            collective_id=0, has_side_effects=True, vmem_limit_bytes=VMEM_BYTES
         ),
     )(
         pick, my_slot, counts, queries.reshape(tiles), keys.reshape(tiles), values.reshape(tiles),

time: 263 us -> 209 us (0.79)
  the two profiles are of different devices: /device:TPU:15 before, /device:TPU:0 now
where the time goes in v2:
time: 209 us; the launch traced here: 206 us
  Pallas kernels  201 us (96%)
  local copies, waits for them, and re-layouts  5.42 us (3%)
    pallas_call x1, Pallas kernels, shards(): pl.pallas_call(functools.partial(layer_kernel, dims, relayed), out_shape=...  201 us

profile of v2, /device:TPU:0, one launch (start us, length us, event | category | flops | bytes accessed | tf_op | source)
XLA Modules:
  0.0 206.4 jit_solution(12129376899991667779)
XLA Ops:
  0.0 0.8 copy.8
  0.8 0.1 reshape.120
  0.9 0.1 convert_reduce_fusion
  1.0 0.2 select_reduce_fusion
  1.2 0.5 dynamic-slice_bitcast_fusion.slot_ref
  1.8 0.6 reshape.121.pick_ref
  2.4 200.6 %shard_map.64 = bf16[1024,1280]{1,0:T(8,128)(2,1)} custom-call(s32[256]{0:T(256)} %reshape.121.pick_ref, s32[32]{0:T(128)} %dynamic-slice_bitcast_fusion.slot_ref, s32[8]{0:T(128)} %count_ref.1, bf16[8,128,640]{2,1,0:T(8,128)(2,1)} %bitcast.5, bf16[8,128,640]{2,1,0:T(8,128)(2,1)} %bitcast.6, bf16[8,128,640]{2,1,0:T(8,128)(2,1)} %bitcast.7, ...), custom_call_target="tpu_custom_call" | custom-call | tf_op jit(solution)/shard_map/pallas_call | solution.py:394
  203.0 3.4 %copy.10 = bf16[1024,1280]{1,0:T(8,128)(2,1)} copy(bf16[1024,1280]{1,0:T(8,128)(2,1)} %shard_map.64) | data formatting | bytes 5242880
  (3 shorter events, 0.0 us)

commit v3 on v2

--- a/solution.py
+++ b/solution.py
@@ -13,6 +13,8 @@
 MESH = pl.DeviceIdType.MESH
 F32 = jnp.float32
 PAIR = 2
+PARTS = 2
+UNROLL = 2
 AHEAD = 2
 VMEM_BYTES = 67043328
 NT_DIMS = (((1,), (1,)), ((), ()))
@@ -77,9 +79,10 @@
             self.build(1)
             self.start(1)
 
-    def receive(self, h):
+    def receive(self, h, midway):
         if h + 2 < self.heads:
             self.build(h + 2)
+        midway()
         self.others(lambda origin: self.copy(h, origin, origin).wait_recv())
         if h + 2 < self.heads:
             self.start(h + 2)
@@ -189,8 +192,10 @@
     def follow(self):
         self.own(0)
 
-    def receive(self, h):
+    def receive(self, h, midway):
         for far in range(1, self.line):
+            if far == self.line - 1:
+                midway()
             self.arrive(h, far)
             if far == 1 and h + AHEAD < self.heads:
                 for way in range(2):
@@ -260,23 +265,63 @@
             device_id_type=MESH,
         )
 
-    def a_copy(h, target, origin):
+    part_blocks = blocks // PARTS
+    part_rows = part_blocks * TILE
+
+    def a_copy(h, part, target, origin):
+        held = attn.at[h, origin, pl.ds(part * part_rows, part_rows)]
         return pltpu.make_async_remote_copy(
-            src_ref=attn.at[h, me_p],
-            dst_ref=attn.at[h, origin],
-            send_sem=a_send.at[h, target],
-            recv_sem=a_recv.at[h, origin],
+            src_ref=held,
+            dst_ref=held,
+            send_sem=a_send.at[h, part, target, origin],
+            recv_sem=a_recv.at[h, part, origin],
             device_id=(me_f, target),
             device_id_type=MESH,
         )
+
+    twin = me_p + 1 - 2 * lax.rem(me_p, 2)
+
+    def over_alike(action):
+        @pl.loop(1, peers // 2)
+        def _(step):
+            action(lax.rem(me_p + 2 * step, peers))
+
+    def over_twins(action):
+        @pl.loop(0, peers // 2)
+        def _(step):
+            action(lax.rem(twin + 2 * step, peers))
+
+    def share(h, part):
+        over_alike(lambda target: a_copy(h, part, target, me_p).start())
+        a_copy(h, part, twin, me_p).start()
+
+    def finish(h):
+        if h == 0:
+            own_rows.wait()
+            over_peers(lambda origin: w_copy(origin, origin).wait_recv())
+        for part in range(PARTS):
+
+            def relay(origin):
+                a_copy(h, part, origin, origin).wait_recv()
+                a_copy(h, part, twin, origin).start()
+
+            over_alike(relay)
+        for part in range(PARTS):
+            over_twins(lambda origin: a_copy(h, part, origin, origin).wait_recv())
+            project(h, part)
+
+    def drain_attn(h, part):
+        over_alike(lambda target: a_copy(h, part, target, me_p).wait_send())
+        a_copy(h, part, twin, me_p).wait_send()
+        over_alike(lambda origin: a_copy(h, part, twin, origin).wait_send())
 
     def over_peers(action):
         @pl.loop(1, peers)
         def _(step):
             action(lax.rem(me_p + step, peers))
 
-    def attend(h):
-        @pl.loop(0, blocks)
+    def attend(h, part):
+        @pl.loop(part * part_blocks, (part + 1) * part_blocks, unroll=UNROLL)
         def _(b):
             q = q_ref[b, :, head_columns(h)]
             picks = [slot_ref[b * select + s] for s in range(select)]
@@ -300,8 +345,8 @@
 
     row_tile = 2 * TILE
 
-    def project(h):
-        @pl.loop(0, blocks * TILE // row_tile)
+    def project(h, part):
+        @pl.loop(part * part_rows // row_tile, (part + 1) * part_rows // row_tile)
         def _(r):
             span = pl.ds(pl.multiple_of(r * row_tile, row_tile), row_tile)
             left = jnp.concatenate([attn[h, p, span, :] for p in range(peers)], axis=1)
@@ -320,21 +365,16 @@
     over_peers(lambda target: w_copy(target, me_p).start())
     exchange.follow()
     for h in range(heads):
-        exchange.receive(h)
-        attend(h)
-        over_peers(lambda target: a_copy(h, target, me_p).start())
-        if h == 0:
-            own_rows.wait()
-            over_peers(lambda origin: w_copy(origin, origin).wait_recv())
-        else:
-            over_peers(lambda origin: a_copy(h - 1, origin, origin).wait_recv())
-            project(h - 1)
-    over_peers(lambda origin: a_copy(heads - 1, origin, origin).wait_recv())
-    project(heads - 1)
+        exchange.receive(h, (lambda: finish(h - 1)) if h > 0 else (lambda: None))
+        for part in range(PARTS):
+            attend(h, part)
+            share(h, part)
+    finish(heads - 1)
     exchange.drain()
     over_peers(lambda target: w_copy(target, me_p).wait_send())
     for h in range(heads):
-        over_peers(lambda target: a_copy(h, target, me_p).wait_send())
+        for part in range(PARTS):
+            drain_attn(h, part)
 
 
 def shards(queries, keys, values, block_ids, counts, w_out):
@@ -371,7 +411,8 @@
         pltpu.VMEM((tokens, features), F32),
     ]
     common_sems = [
-        dma((peers,)), dma((peers,)), dma((heads, peers)), dma((heads, peers)), dma,
+        dma((peers,)), dma((peers,)), dma((heads, PARTS, peers, peers)),
+        dma((heads, PARTS, peers)), dma,
     ]
     recv = [pltpu.VMEM((frames * capacity, 2, TILE, DH), bf16)] * heads
     picked = pltpu.VMEM((heads, line, capacity, 2, TILE, DH), bf16)

time: 209 us -> 205 us (0.981); the launches traced: 206 us -> 205 us
  no operation moved by 1% of the time
where the time goes in v3:
time: 205 us
  Pallas kernels  199 us (97%)
  local copies, waits for them, and re-layouts  5.42 us (3%)
    pallas_call x1, Pallas kernels, shards(): pl.pallas_call(functools.partial(layer_kernel, dims, relayed), out_shape=...  199 us
    unnamed x2, local copies, waits for them, and re-layouts  4.17 us

profile of v3, /device:TPU:0, one launch (start us, length us, event | category | flops | bytes accessed | tf_op | source)
XLA Modules:
  0.0 205.2 jit_solution(11120047719102744846)
XLA Ops:
  0.0 0.8 copy.8
  0.8 0.1 reshape.120
  0.9 0.1 convert_reduce_fusion
  1.0 0.2 select_reduce_fusion
  1.2 0.5 dynamic-slice_bitcast_fusion.slot_ref
  1.8 0.6 reshape.121.pick_ref
  2.4 199.4 %shard_map.64 = bf16[1024,1280]{1,0:T(8,128)(2,1)} custom-call(s32[256]{0:T(256)} %reshape.121.pick_ref, s32[32]{0:T(128)} %dynamic-slice_bitcast_fusion.slot_ref, s32[8]{0:T(128)} %count_ref.1, bf16[8,128,640]{2,1,0:T(8,128)(2,1)} %bitcast.5, bf16[8,128,640]{2,1,0:T(8,128)(2,1)} %bitcast.6, bf16[8,128,640]{2,1,0:T(8,128)(2,1)} %bitcast.7, ...), custom_call_target="tpu_custom_call" | custom-call | tf_op jit(solution)/shard_map/pallas_call | solution.py:435
  201.8 3.4 %copy.10 = bf16[1024,1280]{1,0:T(8,128)(2,1)} copy(bf16[1024,1280]{1,0:T(8,128)(2,1)} %shard_map.64) | data formatting | bytes 5242880
  (3 shorter events, 0.0 us)
